TPU v7x, 128 devices: a whole 4x4x4 slice. The times are simulated.
128 devices in a mesh: ga: 16 (over x, z), band: 8 (over y, core).
Axes of the slice: x: 4, y: 4, z: 4, core: 2. Of those that a mesh axis runs over, the one named last changes fastest.
Arguments:
- coeffs: bfloat16 [2, 2048, 40960], P(None, ('ga', 'band')), may hold values from -6 to 6
- projectors: bfloat16 [1280, 2, 40960], P(None, None, 'ga'), may hold values from -0.01953125 to 0.01953125
- block_coupling: float32 [1280, 18], replicated, may hold values from -12 to 12
- atom_counts: int32 [160], replicated, may hold values from 4 to 18, as said below
- wave_counts: int32 [16], P('ga'), may hold values from 1920 to 2560
Outputs:
- applied: bfloat16 [2, 2048, 40960], P(None, ('ga', 'band'))
- band_energy: float32 [2048], P(('ga', 'band'))
- total_energy: float32 [], replicated
Inputs may be any that keep to these rules, and one draw needn't show every extreme that they name: `atom_counts`: each atom has 4, 8 or 18 projectors, the counts sum to 1280 and the largest is 18.
All inputs are finite; a program needn't handle non-finite values.
Results may differ from a plain program's by a relative error of at most 0.013.
Values may be sent and summed in bfloat16 or wider, within the bound.
A program may use at most 128 MiB of HBM per device.

v0:
```python
import math

import jax
import jax.numpy as jnp
from jax import lax
from jax.sharding import Mesh
from jax.sharding import PartitionSpec as P

GA = ("ga_0", "ga_1")
GA_BAND = ("ga_0", "ga_1", "band_0", "band_1")
BAND = ("band_0", "band_1")


def in_blocks(shard, dim, length):
    before, after = (shard.shape[:dim], shard.shape[dim + 1 :])
    return jnp.moveaxis(shard.reshape(*before, length, -1, *after), dim, 0)


def edges_of(length, count):
    lap = length // count
    if lap >= 8:
        lap -= lap % 8
    return [lap * k for k in range(1, count)]


def laid_out(blocks, dim):
    lengths = list(blocks.shape[1:])
    lengths[dim] *= blocks.shape[0]
    return jnp.moveaxis(blocks, 0, dim).reshape(lengths)


def cut_exchange(shard, axis, pieces, split_dim, concat_dim):
    blocks = in_blocks(shard, split_dim, lax.axis_size(axis))
    cut = max(range(1, max(2, blocks.ndim - 1)), key=lambda d: blocks.shape[d])
    outs = []
    for slab in jnp.split(blocks, edges_of(blocks.shape[cut], pieces), axis=cut):
        if slab.size:
            outs.append(lax.all_to_all(slab, axis, split_axis=0, concat_axis=0, tiled=True))
    return laid_out(jnp.concatenate(outs, axis=cut), concat_dim)


def summed_on_arrival(shard, axis, dim):
    length = lax.axis_size(axis)
    blocks = lax.all_to_all(in_blocks(shard, dim, length), axis, 0, 0, tiled=True)
    return jnp.sum(blocks, axis=0)


def extended_2(cells, sides, width):
    for axis, dim in sides:
        count = lax.axis_size(axis)
        ends = count - 1
        head = lax.slice_in_dim(cells, 0, width, axis=dim)
        tail = lax.slice_in_dim(cells, cells.shape[dim] - width, cells.shape[dim], axis=dim)
        cells = jnp.concatenate(
            [
                lax.ppermute(tail, axis, [(i, (i + 1) % count) for i in range(ends)]),
                cells,
                lax.ppermute(head, axis, [((i + 1) % count, i) for i in range(ends)]),
            ],
            axis=dim,
        )
    return cells


def over_axes(shard, axes):
    for axis in axes:
        shard = lax.psum(shard, axis)
    return shard


def sent_to_all(shard, axis):
    length = lax.axis_size(axis)
    return lax.all_to_all(
        jnp.broadcast_to(shard[None], (length, *shard.shape)), axis, 0, 0, tiled=True
    )


def gathered_copies(shard, axis, dim):
    blocks = sent_to_all(shard, axis)
    return laid_out(blocks, dim)


def block_tables(atom_counts, row_ids):
    atom_ends = jnp.cumsum(atom_counts)
    atom_starts = atom_ends - atom_counts
    inside = (atom_starts[None, :] <= row_ids[:, None]) & (atom_ends[None, :] > row_ids[:, None])
    block_first = jnp.sum(jnp.where(inside, atom_starts[None, :], 0), axis=1)
    block_length = jnp.sum(jnp.where(inside, atom_counts[None, :], 0), axis=1)
    return (block_first, block_length)


def coupling_matrix(block_first, block_length, coupling_rows, column_base, column_count):
    column_ids = column_base + lax.iota(jnp.int32, column_count)
    offsets = column_ids[None, :] - block_first[:, None]
    matrix = jnp.zeros((coupling_rows.shape[0], column_count), jnp.float32)
    for offset in range(coupling_rows.shape[1]):
        hit = (offsets == offset) & (offset < block_length[:, None])
        matrix = jnp.where(hit, coupling_rows[:, offset : offset + 1], matrix)
    return matrix


def shards(coeffs, projectors, block_coupling, atom_counts, wave_counts):
    moved_bands = cut_exchange(coeffs, GA, 2, 2, 1)
    own_bands = coeffs.shape[1]
    group_bands = moved_bands.shape[1]
    wave_slots = projectors.shape[2]
    proj_total_rows = projectors.shape[0]
    in_sphere = (lax.iota(jnp.int32, wave_slots) < wave_counts[0]).astype(jnp.float32)
    masked = moved_bands * in_sphere.astype(jnp.bfloat16)
    real_part = masked[0]
    imag_part = masked[1]
    stacked = jnp.concatenate(
        [jnp.concatenate([real_part, imag_part], 1), jnp.concatenate([imag_part, -real_part], 1)], 0
    )
    flat_beta = projectors.reshape(proj_total_rows, 2 * wave_slots)
    contract_last = (((1,), (1,)), ((), ()))
    contract_first = (((0,), (0,)), ((), ()))
    ga_index = lax.axis_index(GA)
    row_count = proj_total_rows // lax.axis_size(GA)
    rows_beta = flat_beta
    shares = summed_on_arrival(
        lax.dot_general(rows_beta, stacked, contract_last, preferred_element_type=jnp.float32),
        GA,
        0,
    )
    reach_rows = block_coupling.shape[1] - 1
    extended = extended_2(shares.astype(jnp.bfloat16), ((GA, 0),), reach_rows).astype(shares.dtype)
    shard_start = ga_index * row_count
    row_ids = shard_start + lax.iota(jnp.int32, row_count)
    block_first, block_length = block_tables(atom_counts, row_ids)
    coupling_rows = lax.dynamic_slice_in_dim(block_coupling, shard_start, row_count, 0)
    matrix = coupling_matrix(
        block_first, block_length, coupling_rows, shard_start - reach_rows, extended.shape[0]
    )
    coupled = jnp.dot(matrix, extended, preferred_element_type=jnp.float32)
    energy_terms = jnp.sum(shares * coupled, axis=0)
    partial_energy = (energy_terms[:group_bands] + energy_terms[group_bands:]) / proj_total_rows
    band_energy = summed_on_arrival(partial_energy, GA, 0)
    total_energy = over_axes(jnp.sum(band_energy), GA_BAND)
    rows_beta = flat_beta
    products = lax.dot_general(
        gathered_copies(coupled.astype(jnp.bfloat16), GA, 0),
        rows_beta,
        contract_first,
        preferred_element_type=jnp.float32,
    )
    band_total = own_bands * lax.axis_size(GA) * lax.axis_size(BAND)
    total_energy = total_energy / math.sqrt(band_total)
    real_out = products[:group_bands, :wave_slots] - products[group_bands:, wave_slots:]
    imag_out = products[:group_bands, wave_slots:] + products[group_bands:, :wave_slots]
    result = (jnp.stack([real_out, imag_out]) * in_sphere).astype(jnp.bfloat16)
    applied = lax.all_to_all(result, GA, split_axis=1, concat_axis=2, tiled=True)
    return (applied, band_energy, total_energy)


def solution(mesh):
    torus = Mesh(mesh.devices.reshape(4, 4, 4, 2), ("ga_0", "ga_1", "band_0", "band_1"))
    return jax.shard_map(
        shards,
        mesh=torus,
        in_specs=(P(None, GA_BAND, None), P(None, None, GA), P(), P(), P(GA)),
        out_specs=(P(None, GA_BAND, None), P(GA_BAND), P()),
        check_vma=False,
    )
```

profile of v0, /device:TPU:0, one launch (start us, length us, event | category | flops | bytes accessed | tf_op | source)
XLA Modules:
  0.0 237.6 jit_solution(8688258007273282612)
XLA Ops:
  0.6 2.5 %copy.38 = bf16[4,8,16,2560]{3,2,1,0:T(8,128)(2,1)S(1)} copy(bf16[4,8,16,2560]{3,1,2,0:T(8,128)(2,1)} %bitcast.87) | data formatting | bytes 5242880
  5.3 8.0 %all-to-all-start = ((bf16[16,2,8,2560]{3,2,1,0:T(8,128)(2,1)}), bf16[16,2,8,2560]{3,2,1,0:T(8,128)(2,1)S(1)}, u32[]{:S(2)}, u32[]{:S(2)}) async-start(bf16[16,2,8,2560]{3,2,1,0:T(8,128)(2,1)} %copy.28), calls=%async_computation | async-start | bytes 2621440 | tf_op jit(solution)/shard_map/all_to_all | solution.py:38
  15.1 19.0 %all-to-all-done = bf16[16,2,8,2560]{3,2,1,0:T(8,128)(2,1)S(1)} async-done(((bf16[16,2,8,2560]{3,2,1,0:T(8,128)(2,1)}), bf16[16,2,8,2560]{3,2,1,0:T(8,128)(2,1)S(1)}, u32[]{:S(2)}, u32[]{:S(2)}) %all-to-all-start) | async-done | bytes 1310752 | tf_op jit(solution)/shard_map/all_to_all | solution.py:38
  34.1 3.7 %all-to-all-start.1 = ((bf16[16,2,8,2560]{3,2,1,0:T(8,128)(2,1)}), bf16[16,2,8,2560]{3,2,1,0:T(8,128)(2,1)S(1)}, u32[]{:S(2)}, u32[]{:S(2)}) async-start(bf16[16,2,8,2560]{3,2,1,0:T(8,128)(2,1)} %copy.29), calls=%async_computation.1 | async-start | bytes 2621440 | tf_op jit(solution)/shard_map/all_to_all | solution.py:38
  38.4 12.2 %copy.39 = bf16[160,8,2,2560]{3,1,2,0:T(8,128)(2,1)} copy(bf16[160,8,2,2560]{3,2,1,0:T(2,128)(2,1)} %bitcast.81) | data formatting | bytes 26214400
  50.6 5.4 %all-to-all-done.1 = bf16[16,2,8,2560]{3,2,1,0:T(8,128)(2,1)S(1)} async-done(((bf16[16,2,8,2560]{3,2,1,0:T(8,128)(2,1)}), bf16[16,2,8,2560]{3,2,1,0:T(8,128)(2,1)S(1)}, u32[]{:S(2)}, u32[]{:S(2)}) %all-to-all-start.1) | async-done | bytes 1310752 | tf_op jit(solution)/shard_map/all_to_all | solution.py:38
  59.6 15.8 %fusion.9 = f32[1280,512]{0,1:T(8,128)S(1)} fusion(bf16[1280,5120]{1,0:T(8,128)(2,1)} %bitcast.82, bf16[256,2560]{1,0:T(8,128)(2,1)} %fusion.154, bf16[256,2560]{1,0:T(8,128)(2,1)} %get-tuple-element.10, bf16[256,2560]{1,0:T(8,128)(2,1)} %get-tuple-element.9), kind=kOutput, calls=%fused_computation.10 | convolution fusion | flops 6731857920 | bytes 19660800 | tf_op jit(solution)/shard_map/dot_general | solution.py:122
  75.4 2.1 copy.32
  77.5 3.9 %all-to-all-start.2 = ((f32[16,80,512]{2,1,0:T(8,128)}), f32[16,80,512]{2,1,0:T(8,128)S(1)}, u32[]{:S(2)}, u32[]{:S(2)}) async-start(f32[16,80,512]{2,1,0:T(8,128)} %bitcast.84), calls=%async_computation.2 | async-start | bytes 5242880 | tf_op jit(solution)/shard_map/all_to_all | solution.py:44
  83.5 31.9 %all-to-all-done.2 = f32[16,80,512]{2,1,0:T(8,128)S(1)} async-done(((f32[16,80,512]{2,1,0:T(8,128)}), f32[16,80,512]{2,1,0:T(8,128)S(1)}, u32[]{:S(2)}, u32[]{:S(2)}) %all-to-all-start.2) | async-done | bytes 2621472 | tf_op jit(solution)/shard_map/all_to_all | solution.py:44
  115.6 2.5 %collective-permute-start = (bf16[17,512]{1,0:T(8,128)(2,1)S(1)}, bf16[17,512]{1,0:T(8,128)(2,1)S(1)}, u32[]{:S(2)}, u32[]{:S(2)}) collective-permute-start(bf16[17,512]{1,0:T(8,128)(2,1)S(1)} %get-tuple-element.33), channel_id=1, source_target_pairs={{0,8},{8,16},{16,24},{24,32},{32,40},{40,48},{48,56},{56,64},{64,7... | collective-permute-start | bytes 52232 | tf_op jit(solution)/shard_map/ppermute | solution.py:56
  119.6 4.2 %collective-permute-done.1 = bf16[17,512]{1,0:T(8,128)(2,1)S(1)} collective-permute-done((bf16[17,512]{1,0:T(8,128)(2,1)S(1)}, bf16[17,512]{1,0:T(8,128)(2,1)S(1)}, u32[]{:S(2)}, u32[]{:S(2)}) %collective-permute-start.1) | collective-permute-done | bytes 17440 | tf_op jit(solution)/shard_map/ppermute | solution.py:58
  125.6 7.7 %all-to-all-start.3 = ((bf16[16,80,512]{2,1,0:T(8,128)(2,1)}), bf16[16,80,512]{2,1,0:T(8,128)(2,1)S(1)}, u32[]{:S(2)}, u32[]{:S(2)}) async-start(bf16[16,80,512]{2,1,0:T(8,128)(2,1)} %broadcast_in_dim.221), calls=%async_computation.3 | async-start | bytes 2621440 | tf_op jit(solution)/shard_map/all_to_all | solution.py:73
  134.0 13.8 %all-to-all-done.3 = bf16[16,80,512]{2,1,0:T(8,128)(2,1)S(1)} async-done(((bf16[16,80,512]{2,1,0:T(8,128)(2,1)}), bf16[16,80,512]{2,1,0:T(8,128)(2,1)S(1)}, u32[]{:S(2)}, u32[]{:S(2)}) %all-to-all-start.3) | async-done | bytes 1310752 | tf_op jit(solution)/shard_map/all_to_all | solution.py:73
  147.8 3.5 %all-to-all-start.5 = ((f32[16,1,16]{2,1,0:T(1,128)}), f32[16,1,16]{2,1,0:T(1,128)S(1)}, u32[]{:S(2)}, u32[]{:S(2)}) async-start(f32[16,1,16]{2,1,0:T(1,128)} %div.13), calls=%async_computation.5 | async-start | bytes 16384 | tf_op jit(solution)/shard_map/all_to_all | solution.py:44
  151.3 10.1 %fusion.158 = f32[512,5120]{1,0:T(8,128)S(1)} fusion(bf16[1280,512]{1,0:T(8,128)(2,1)S(1)} %bitcast.88, bf16[1280,5120]{1,0:T(8,128)(2,1)} %bitcast.83), kind=kOutput, calls=%fused_computation.212 | convolution fusion | flops 6710886400 | bytes 24903680 | tf_op jit(solution)/shard_map/dot_general | solution.py:141
  162.9 4.2 %copy.33 = bf16[2,256,2560]{2,0,1:T(2,128)(2,1)} copy(bf16[2,256,2560]{2,1,0:T(8,128)(2,1)S(1)} %fusion.8) | data formatting | bytes 5242880 | tf_op jit(solution)/shard_map/convert_element_type | solution.py:151
  167.1 7.2 %all-to-all-start.4 = ((bf16[2,256,2560]{2,0,1:T(2,128)(2,1)}), bf16[2,256,2560]{2,0,1:T(2,128)(2,1)S(1)}, u32[]{:S(2)}, u32[]{:S(2)}) async-start(bf16[2,256,2560]{2,0,1:T(2,128)(2,1)} %copy.33), calls=%async_computation.4 | async-start | bytes 5242880 | tf_op jit(solution)/shard_map/all_to_all | solution.py:152
  175.0 29.0 %psum.28 = f32[]{:T(128)} all-reduce(f32[]{:T(128)} %get-tuple-element.3), channel_id=1, replica_groups=mesh['ga_0'=4,'ga_1'=4,'band_0'=4,'band_1'=2] {'ga_0'}, use_global_device_ids=true, to_apply=%region_8.9 | all-reduce | flops 1 | bytes 8 | tf_op jit(solution)/shard_map/psum | solution.py:67
  204.0 10.0 %psum.29 = f32[]{:T(128)} all-reduce(f32[]{:T(128)} %psum.28), channel_id=1, replica_groups=mesh['ga_0'=4,'ga_1'=4,'band_0'=4,'band_1'=2] {'ga_1'}, use_global_device_ids=true, to_apply=%region_9.10 | all-reduce | flops 1 | bytes 8 | tf_op jit(solution)/shard_map/psum | solution.py:67
  214.0 11.3 %psum.30 = f32[]{:T(128)} all-reduce(f32[]{:T(128)} %psum.29), channel_id=1, replica_groups=mesh['ga_0'=4,'ga_1'=4,'band_0'=4,'band_1'=2] {'band_0'}, use_global_device_ids=true, to_apply=%region_10.11 | all-reduce | flops 1 | bytes 8 | tf_op jit(solution)/shard_map/psum | solution.py:67
  225.3 3.1 %psum.31 = f32[]{:T(128)} all-reduce(f32[]{:T(128)} %psum.30), channel_id=1, replica_groups=mesh['ga_0'=4,'ga_1'=4,'band_0'=4,'band_1'=2] {'band_1'}, use_global_device_ids=true, to_apply=%region_11.12 | all-reduce | flops 1 | bytes 8 | tf_op jit(solution)/shard_map/psum | solution.py:67
  229.0 2.9 %copy.34 = bf16[2,16,16,2560]{3,2,1,0:T(8,128)(2,1)} copy(bf16[2,16,16,2560]{3,0,1,2:T(2,128)(2,1)S(1)} %bitcast.85) | data formatting | bytes 5242880 | tf_op jit(solution)/shard_map/all_to_all | solution.py:152
  232.0 4.5 %all_to_all.36 = bf16[2,16,40960]{2,1,0:T(8,128)(2,1)} reshape(bf16[2,16,16,2560]{3,2,1,0:T(8,128)(2,1)} %copy.34) | data formatting | bytes 5242880 | tf_op jit(solution)/shard_map/all_to_all | solution.py:152
  (39 shorter events, 15.8 us)
Async XLA Ops:
  5.3 28.8 %all-to-all-start = ((bf16[16,2,8,2560]{3,2,1,0:T(8,128)(2,1)}), bf16[16,2,8,2560]{3,2,1,0:T(8,128)(2,1)S(1)}, u32[]{:S(2)}, u32[]{:S(2)}) async-start(bf16[16,2,8,2560]{3,2,1,0:T(8,128)(2,1)} %copy.28), calls=%async_computation | async-start | bytes 2621440 | tf_op jit(solution)/shard_map/all_to_all | solution.py:38
  34.1 21.9 %all-to-all-start.1 = ((bf16[16,2,8,2560]{3,2,1,0:T(8,128)(2,1)}), bf16[16,2,8,2560]{3,2,1,0:T(8,128)(2,1)S(1)}, u32[]{:S(2)}, u32[]{:S(2)}) async-start(bf16[16,2,8,2560]{3,2,1,0:T(8,128)(2,1)} %copy.29), calls=%async_computation.1 | async-start | bytes 2621440 | tf_op jit(solution)/shard_map/all_to_all | solution.py:38
  77.5 3.9 %copy-start = (s32[160]{0:T(256)S(1)}, s32[160]{0:T(256)}, u32[]{:S(2)}) copy-start(s32[160]{0:T(256)} %param.8) | copy-start | bytes 1924
  77.5 37.8 %all-to-all-start.2 = ((f32[16,80,512]{2,1,0:T(8,128)}), f32[16,80,512]{2,1,0:T(8,128)S(1)}, u32[]{:S(2)}, u32[]{:S(2)}) async-start(f32[16,80,512]{2,1,0:T(8,128)} %bitcast.84), calls=%async_computation.2 | async-start | bytes 5242880 | tf_op jit(solution)/shard_map/all_to_all | solution.py:44
  115.6 4.0 %collective-permute-start = (bf16[17,512]{1,0:T(8,128)(2,1)S(1)}, bf16[17,512]{1,0:T(8,128)(2,1)S(1)}, u32[]{:S(2)}, u32[]{:S(2)}) collective-permute-start(bf16[17,512]{1,0:T(8,128)(2,1)S(1)} %get-tuple-element.33), channel_id=1, source_target_pairs={{0,8},{8,16},{16,24},{24,32},{32,40},{40,48},{48,56},{56,64},{64,7... | collective-permute-start | bytes 52232 | tf_op jit(solution)/shard_map/ppermute | solution.py:56
  118.1 5.7 %collective-permute-start.1 = (bf16[17,512]{1,0:T(8,128)(2,1)S(1)}, bf16[17,512]{1,0:T(8,128)(2,1)S(1)}, u32[]{:S(2)}, u32[]{:S(2)}) collective-permute-start(bf16[17,512]{1,0:T(8,128)(2,1)S(1)} %get-tuple-element.34), channel_id=1, source_target_pairs={{8,0},{16,8},{24,16},{32,24},{40,32},{48,40},{56,48},{64,56},{72,6... | collective-permute-start | bytes 52232 | tf_op jit(solution)/shard_map/ppermute | solution.py:58
  125.6 22.2 %all-to-all-start.3 = ((bf16[16,80,512]{2,1,0:T(8,128)(2,1)}), bf16[16,80,512]{2,1,0:T(8,128)(2,1)S(1)}, u32[]{:S(2)}, u32[]{:S(2)}) async-start(bf16[16,80,512]{2,1,0:T(8,128)(2,1)} %broadcast_in_dim.221), calls=%async_computation.3 | async-start | bytes 2621440 | tf_op jit(solution)/shard_map/all_to_all | solution.py:73
  147.8 19.3 %all-to-all-start.5 = ((f32[16,1,16]{2,1,0:T(1,128)}), f32[16,1,16]{2,1,0:T(1,128)S(1)}, u32[]{:S(2)}, u32[]{:S(2)}) async-start(f32[16,1,16]{2,1,0:T(1,128)} %div.13), calls=%async_computation.5 | async-start | bytes 16384 | tf_op jit(solution)/shard_map/all_to_all | solution.py:44
  167.1 61.9 %all-to-all-start.4 = ((bf16[2,256,2560]{2,0,1:T(2,128)(2,1)}), bf16[2,256,2560]{2,0,1:T(2,128)(2,1)S(1)}, u32[]{:S(2)}, u32[]{:S(2)}) async-start(bf16[2,256,2560]{2,0,1:T(2,128)(2,1)} %copy.33), calls=%async_computation.4 | async-start | bytes 5242880 | tf_op jit(solution)/shard_map/all_to_all | solution.py:152
where the time goes:
time: 240 us; the launch traced here: 238 us
  waiting for transfers between devices  74.3 us (31%)
  blocking collectives  53.4 us (22%)
  starting transfers between devices  38 us (16%)
  local copies, waits for them, and re-layouts  37.4 us (16%)
  matrix products  26.5 us (11%)
  other arithmetic  4.75 us (2%)
  between operations  3.31 us (1%)
    psum x4, blocking collectives, over_axes(): shard = lax.psum(shard, axis)  53.4 us
    all_to_all x2, waiting for transfers between devices, summed_on_arrival(): lax.all_to_all(in_blocks(shard, dim, length), axis, 0, 0, tiled=True)  31.9 us
    all_to_all x2, waiting for transfers between devices, cut_exchange(): lax.all_to_all(slab, axis, split_axis=0, concat_axis=0, tiled=True)  24.4 us
    dot_general x1, matrix products, shards(): lax.dot_general(rows_beta, stacked, contract_last, preferred_element_type...  15.8 us
    unnamed x4, local copies, waits for them, and re-layouts  14.7 us
    all_to_all x1, waiting for transfers between devices, sent_to_all(): lax.all_to_all(jnp.broadcast_to(shard[None], (length, *shard.shape)), axi...  13.8 us
    all_to_all x2, starting transfers between devices, cut_exchange(): lax.all_to_all(slab, axis, split_axis=0, concat_axis=0, tiled=True)  11.7 us
    dot_general x1, matrix products, shards(): lax.dot_general(gathered_copies(coupled.astype(jnp.bfloat16), GA, 0), row...  10.1 us
  transfers between devices with their start and end apart: 8, of which 5 were waited for; matrix products, arithmetic and copies ran while one was open for 14% of the time, Pallas kernels for 0%

commit v1 on v0

v1 whole, which is shorter than its diff:
```python
import math

import jax
import jax.numpy as jnp
from jax import lax
from jax.experimental import pallas as pl
from jax.experimental.pallas import tpu as pltpu
from jax.sharding import PartitionSpec as P

MESH = pl.DeviceIdType.MESH
SIDE = 4
GROUP = 4
REACH = 17

PLACES = [(0, 0)] + sorted(
    [(dx, dz) for dx in range(SIDE) for dz in range(SIDE) if (dx, dz) != (0, 0)],
    key=lambda o: min(o[0], SIDE - o[0]) + min(o[1], SIDE - o[1]),
)


def kernel(
    counts_ref,
    waves_ref,
    coupling_ref,
    coeffs_ref,
    proj_ref,
    out_ref,
    energy_ref,
    total_ref,
    beta,
    moved,
    lhs,
    part,
    parts_in,
    mixed,
    mixed_in,
    prod,
    weights,
    mask,
    own_energy,
    energy_in,
    group_energy,
    band_in,
    beta_sem,
    own_sem,
    in_sems,
    part_sems,
    mixed_sems,
    out_sems,
    energy_sems,
    band_sems,
):
    n_ga = len(PLACES)
    n_band = lax.axis_size("band")
    own = mixed.shape[0]
    slots = moved.shape[2]
    rows = beta.shape[0]
    tile = 256
    ga = lax.axis_index("ga")
    band = lax.axis_index("band")
    gx, gz = ga // SIDE, ga % SIDE

    def ahead(n):
        dx, dz = PLACES[n]
        return lax.rem(gx + dx, SIDE) * SIDE + lax.rem(gz + dz, SIDE)

    def behind(n):
        dx, dz = PLACES[n]
        return lax.rem(gx + SIDE - dx, SIDE) * SIDE + lax.rem(gz + SIDE - dz, SIDE)

    def columns(index):
        return pl.ds(pl.multiple_of(index * slots, 128), slots)

    def send(src, dst, sems, n, target):
        return pltpu.make_async_remote_copy(
            src, dst, sems.at[0, n], sems.at[1, n], device_id=target, device_id_type=MESH
        )

    beta_copy = pltpu.make_async_copy(proj_ref.reshape(rows, slots), beta, beta_sem)
    own_copy = pltpu.make_async_copy(coeffs_ref.at[:, columns(ga)], moved.at[0], own_sem.at[0])
    own_copy.start()

    barrier = pltpu.get_barrier_semaphore()
    for n in range(1, n_ga):
        pl.semaphore_signal(barrier, inc=1, device_id={"ga": ahead(n)}, device_id_type=MESH)
    for n in range(1, n_band):
        target = {"band": lax.rem(band + n, n_band)}
        pl.semaphore_signal(barrier, inc=1, device_id=target, device_id_type=MESH)
    pl.semaphore_wait(barrier, n_ga + n_band - 2)

    in_copies = [None]
    for n in range(1, n_ga):
        peer = ahead(n)
        in_copies.append(
            send(coeffs_ref.at[:, columns(peer)], moved.at[n], in_sems, n, {"ga": peer})
        )
        in_copies[n].start()
    beta_copy.start()

    slot_ids = lax.broadcasted_iota(jnp.int32, mask.shape, 1)
    mask[...] = jnp.where(slot_ids < waves_ref[0], 1.0, 0.0)
    atoms = counts_ref.shape[1]
    counts = jnp.broadcast_to(counts_ref[...], (atoms, atoms))
    lane_ids = lax.broadcasted_iota(jnp.int32, (atoms, atoms), 1)
    row_ids = lax.broadcasted_iota(jnp.int32, (atoms, atoms), 0)
    starts = jnp.sum(jnp.where(lane_ids < row_ids, counts, 0.0), axis=1, keepdims=True)
    lengths = jnp.sum(jnp.where(lane_ids == row_ids, counts, 0.0), axis=1, keepdims=True)
    most = coupling_ref.shape[0]
    half = tile // 2
    spread = jnp.where(
        lax.broadcasted_iota(jnp.int32, (half, tile), 1) // 2
        == lax.broadcasted_iota(jnp.int32, (half, tile), 0),
        1.0,
        0.0,
    )

    def weights_of(t, carry):
        at = pl.ds(pl.multiple_of(t * tile, tile), tile)
        halved = coupling_ref[:, pl.ds(pl.multiple_of(t * half, half), half)]
        pairs = jnp.dot(
            halved, spread, precision=lax.Precision.HIGHEST, preferred_element_type=jnp.float32
        )
        ids = t * half + lax.broadcasted_iota(jnp.int32, (atoms, tile), 1) // 2
        ids = ids.astype(jnp.float32)
        inside = (starts <= ids) & (ids < starts + lengths)
        first = jnp.sum(jnp.where(inside, starts, 0.0), axis=0, keepdims=True)
        length = jnp.sum(jnp.where(inside, lengths, 0.0), axis=0, keepdims=True)
        shape = (weights.shape[0], tile)
        shift = lax.broadcasted_iota(jnp.int32, shape, 0).astype(jnp.float32) - REACH
        place = shift + (ids[0:1] - first)
        sums = jnp.zeros(shape, jnp.float32)
        for k in range(most):
            row = jnp.where(k < length, pairs[k : k + 1], 0.0)
            sums = sums + jnp.where(place == k, row, 0.0)
        weights[:, at] = sums
        return carry

    lax.fori_loop(0, rows // tile, weights_of, 0)

    def even_lanes(shape):
        return lax.broadcasted_iota(jnp.int32, shape, len(shape) - 1) % 2 == 0

    def swapped(values, even):
        last = values.shape[-1]
        dim = len(values.shape) - 1
        return jnp.where(even, pltpu.roll(values, last - 1, dim), pltpu.roll(values, 1, dim))

    beta_copy.wait()
    part_copies = [None] * n_ga
    for first in range(0, n_ga, GROUP):
        for n in range(first, first + GROUP):
            if n == 0:
                own_copy.wait()
            else:
                in_copies[n].wait_recv()
        seen = mask[0:1, :].astype(jnp.bfloat16)
        lhs[...] = moved[first : first + GROUP].reshape(lhs.shape) * seen

        def project(t, carry):
            at = pl.ds(pl.multiple_of(t * tile, tile), tile)
            sums = lax.dot_general(
                lhs[...],
                beta[at, :],
                (((1,), (1,)), ((), ())),
                preferred_element_type=jnp.float32,
            )
            even = even_lanes((own, tile))
            for k in range(GROUP):
                real = sums[2 * own * k : 2 * own * k + own]
                imag = sums[2 * own * k + own : 2 * own * (k + 1)]
                pairs = jnp.where(even, real, -real) + swapped(imag, even)
                part[first + k, :, at] = pairs.astype(jnp.bfloat16)
            return carry

        lax.fori_loop(0, rows // tile, project, 0)
        for n in range(max(first, 1), first + GROUP):
            part_copies[n] = send(part.at[n], parts_in.at[n], part_sems, n, {"ga": behind(n)})
            part_copies[n].start()

    summed = part[0].astype(jnp.float32)
    for n in range(1, n_ga):
        part_copies[n].wait_recv()
        summed = summed + parts_in[n].astype(jnp.float32)
    coupled = jnp.zeros_like(summed)
    for d in range(-REACH, REACH + 1):
        moved_by = pltpu.roll(summed, (-2 * d) % rows, 1) if d else summed
        coupled = coupled + weights[d + REACH : d + REACH + 1, :] * moved_by
    mixed[...] = coupled.astype(jnp.bfloat16)
    mixed_in[0] = mixed[...]
    mixed_copies = [None]
    for n in range(1, n_ga):
        mixed_copies.append(send(mixed, mixed_in.at[n], mixed_sems, n, {"ga": ahead(n)}))
        mixed_copies[n].start()
    terms = jnp.sum(summed * coupled, axis=1, keepdims=True) / (rows // 2)
    diagonal = lax.broadcasted_iota(jnp.int32, (own, 128), 0) == lax.broadcasted_iota(
        jnp.int32, (own, 128), 1
    )
    terms_row = jnp.sum(jnp.where(diagonal, terms, 0.0), axis=0, keepdims=True)
    energy_ref[...] = terms_row
    own_energy[...] = jnp.broadcast_to(jnp.sum(terms, axis=0, keepdims=True), own_energy.shape)
    energy_copies = []
    for n in range(1, n_ga):
        energy_copies.append(
            send(own_energy, energy_in.at[ga], energy_sems, n, {"ga": ahead(n)})
        )
        energy_copies[-1].start()

    out_copies = [None] * n_ga
    for first in range(0, n_ga, GROUP):
        for n in range(max(first, 1), first + GROUP):
            mixed_copies[n].wait_recv()
        even = even_lanes((own, rows))
        for k in range(GROUP):
            values = mixed_in[first + k].astype(jnp.float32)
            lhs[2 * own * k : 2 * own * k + own, :] = jnp.where(even, values, -values).astype(
                jnp.bfloat16
            )
            lhs[2 * own * k + own : 2 * own * (k + 1), :] = swapped(values, even).astype(
                jnp.bfloat16
            )

        def apply(t, carry):
            at = pl.ds(pl.multiple_of(t * tile, tile), tile)
            sums = jnp.dot(lhs[...], beta[:, at], preferred_element_type=jnp.float32)
            sums = sums * mask[0:1, at]
            prod[first : first + GROUP, :, at] = sums.astype(jnp.bfloat16).reshape(
                GROUP, 2 * own, tile
            )
            return carry

        lax.fori_loop(0, slots // tile, apply, 0)
        for n in range(first, first + GROUP):
            place = out_ref.at[:, columns(ga)]
            if n == 0:
                out_copies[0] = pltpu.make_async_copy(prod.at[0], place, own_sem.at[1])
            else:
                out_copies[n] = send(prod.at[n], place, out_sems, n, {"ga": behind(n)})
            out_copies[n].start()

    for copy in energy_copies:
        copy.wait_recv()
    energy_in[pl.ds(ga, 1)] = own_energy[...][None]
    sums = energy_in[0]
    for n in range(1, n_ga):
        sums = sums + energy_in[n]
    group_energy[...] = sums
    band_copies = []
    for n in range(1, n_band):
        target = {"band": lax.rem(band + n, n_band)}
        band_copies.append(send(group_energy, band_in.at[band], band_sems, n, target))
        band_copies[-1].start()
    for copy in band_copies:
        copy.wait_recv()
    band_in[pl.ds(band, 1)] = sums[None]
    sums = band_in[0]
    for n in range(1, n_band):
        sums = sums + band_in[n]
    total_ref[...] = sums / math.sqrt(own * n_ga * n_band)

    for n in range(n_ga):
        if n == 0:
            out_copies[0].wait()
        else:
            out_copies[n].wait_recv()
    for n in range(1, n_ga):
        in_copies[n].wait_send()
        part_copies[n].wait_send()
        mixed_copies[n].wait_send()
        energy_copies[n - 1].wait_send()
        out_copies[n].wait_send()
    for copy in band_copies:
        copy.wait_send()


def shards(coeffs, projectors, block_coupling, atom_counts, wave_counts):
    parts, own, slots_all = coeffs.shape
    rows = projectors.shape[0] * parts
    slots = projectors.shape[2]
    n_ga = lax.axis_size("ga")
    n_band = lax.axis_size("band")
    low, full = jnp.bfloat16, jnp.float32
    vmem = pl.BlockSpec(memory_space=pltpu.VMEM)
    anywhere = pl.BlockSpec(memory_space=pl.ANY)
    applied, energy, total = pl.pallas_call(
        kernel,
        out_shape=[
            jax.ShapeDtypeStruct((parts * own, slots_all), low),
            jax.ShapeDtypeStruct((1, 128), full),
            jax.ShapeDtypeStruct((8, 128), full),
        ],
        in_specs=[vmem, pl.BlockSpec(memory_space=pltpu.SMEM), vmem, anywhere, anywhere],
        out_specs=[anywhere, vmem, vmem],
        scratch_shapes=[
            pltpu.VMEM((rows, slots), low),
            pltpu.VMEM((n_ga, parts * own, slots), low),
            pltpu.VMEM((GROUP * parts * own, slots), low),
            pltpu.VMEM((n_ga, own, rows), low),
            pltpu.VMEM((n_ga, own, rows), low),
            pltpu.VMEM((own, rows), low),
            pltpu.VMEM((n_ga, own, rows), low),
            pltpu.VMEM((n_ga, parts * own, slots), low),
            pltpu.VMEM((40, rows), full),
            pltpu.VMEM((8, slots), full),
            pltpu.VMEM((8, 128), full),
            pltpu.VMEM((n_ga, 8, 128), full),
            pltpu.VMEM((8, 128), full),
            pltpu.VMEM((n_band, 8, 128), full),
            pltpu.SemaphoreType.DMA,
            pltpu.SemaphoreType.DMA((2,)),
            pltpu.SemaphoreType.DMA((2, n_ga)),
            pltpu.SemaphoreType.DMA((2, n_ga)),
            pltpu.SemaphoreType.DMA((2, n_ga)),
            pltpu.SemaphoreType.DMA((2, n_ga)),
            pltpu.SemaphoreType.DMA((2, n_ga)),
            pltpu.SemaphoreType.DMA((2, n_band)),
        ],
        compiler_params=pltpu.CompilerParams(
            collective_id=0, has_side_effects=True, vmem_limit_bytes=56 << 20
        ),
    )(
        atom_counts.astype(full).reshape(1, -1),
        wave_counts,
        block_coupling.T,
        coeffs.reshape(parts * own, slots_all),
        projectors,
    )
    return applied.reshape(coeffs.shape), energy[0, :own], total[0, 0]


def solution(mesh):
    return jax.shard_map(
        shards,
        mesh=mesh,
        in_specs=(P(None, ("ga", "band"), None), P(None, None, "ga"), P(), P(), P("ga")),
        out_specs=(P(None, ("ga", "band"), None), P(("ga", "band")), P()),
        check_vma=False,
    )
```

time: 240 us -> 131 us (0.55)
  the two profiles are of different devices: /device:TPU:0 before, /device:TPU:14 now
where the time goes in v1:
time: 131 us
  Pallas kernels  123 us (94%)
  local copies, waits for them, and re-layouts  5.7 us (4%)
    pallas_call x1, Pallas kernels, shards(): pl.pallas_call(kernel, out_shape=[jax.ShapeDtypeStruct((parts * own, slot...  123 us
    unnamed x1, local copies, waits for them, and re-layouts  3.4 us

profile of v1, /device:TPU:14, one launch (start us, length us, event | category | flops | bytes accessed | tf_op | source)
XLA Modules:
  0.0 131.2 jit_solution(1028969193396035903)
XLA Ops:
  1.3 1.2 convert_element_type.3
  2.5 122.9 %shard_map.76 = (bf16[32,40960]{1,0:T(8,128)(2,1)}, f32[1,128]{1,0:T(1,128)}, f32[8,128]{1,0:T(8,128)}) custom-call(f32[1,160]{1,0:T(1,128)} %bitcast.10, s32[1]{0:T(128)S(6)} %copy.9.waves_ref, f32[18,1280]{1,0:T(8,128)} %bitcast.9, bf16[32,40960]{1,0:T(8,128)(2,1)} %bitcast.8, bf16[1280,2,2560]{2,1,0:T(2,128)(2,1)} %proj_ref.1), custom_call_target="tpu_custom_call" | custom-call | tf_op jit(solution)/shard_map/pallas_call | solution.py:284
  125.5 1.2 slice.7
  126.7 1.1 slice_bitcast_fusion
  127.8 3.4 %copy.10 = bf16[2,16,40960]{2,1,0:T(8,128)(2,1)} copy(bf16[2,16,40960]{2,1,0:T(8,128)(2,1)} %bitcast.7) | data formatting | bytes 5242880

commit v2 on v1

v2 whole, which is shorter than its diff:
```python
import math

import jax
import jax.numpy as jnp
from jax import lax
from jax.experimental import pallas as pl
from jax.experimental.pallas import tpu as pltpu
from jax.sharding import PartitionSpec as P

MESH = pl.DeviceIdType.MESH
SIDE = 4
REACH = 17

PLACES = [(0, 0)] + sorted(
    [(dx, dz) for dx in range(SIDE) for dz in range(SIDE) if (dx, dz) != (0, 0)],
    key=lambda o: min(o[0], SIDE - o[0]) + min(o[1], SIDE - o[1]),
)


def kernel(
    counts_ref,
    waves_ref,
    coupling_ref,
    coeffs_ref,
    proj_ref,
    out_ref,
    energy_ref,
    total_ref,
    beta,
    moved,
    lhs,
    part,
    parts_in,
    mixed,
    mixed_in,
    prod,
    weights,
    mask,
    own_energy,
    energy_in,
    group_energy,
    band_in,
    beta_sem,
    own_sem,
    in_sems,
    part_sems,
    mixed_sems,
    out_sems,
    energy_sems,
    band_sems,
):
    n_ga = len(PLACES)
    n_band = lax.axis_size("band")
    half = mixed.shape[1]
    own = 2 * half
    slots = moved.shape[3]
    rows = beta.shape[0]
    tile = 256
    ga = lax.axis_index("ga")
    band = lax.axis_index("band")
    gx, gz = ga // SIDE, ga % SIDE

    def ahead(n):
        dx, dz = PLACES[n]
        return lax.rem(gx + dx, SIDE) * SIDE + lax.rem(gz + dz, SIDE)

    def behind(n):
        dx, dz = PLACES[n]
        return lax.rem(gx + SIDE - dx, SIDE) * SIDE + lax.rem(gz + SIDE - dz, SIDE)

    def columns(index):
        return pl.ds(pl.multiple_of(index * slots, 128), slots)

    def send(src, dst, sems, at, target):
        return pltpu.make_async_remote_copy(
            src,
            dst,
            sems.at[(0, *at)],
            sems.at[(1, *at)],
            device_id=target,
            device_id_type=MESH,
        )

    flat_proj = proj_ref.reshape(rows, slots)
    beta_copy = pltpu.make_async_copy(flat_proj, beta, beta_sem)

    def load_beta(t, carry):
        at = pl.ds(pl.multiple_of(t * tile, tile), tile)
        pltpu.make_async_copy(flat_proj.at[at], beta.at[at], beta_sem).start()
        return carry

    lax.fori_loop(0, rows // tile, load_beta, 0)

    def bands(h, c):
        return pl.ds(c * own + h * half, half)

    def part_rows(c):
        return pl.ds(c * half, half)

    own_copies = []
    for h in range(2):
        for c in range(2):
            own_copies.append(
                pltpu.make_async_copy(
                    coeffs_ref.at[bands(h, c), columns(ga)],
                    moved.at[h, 0, part_rows(c)],
                    own_sem.at[h, c],
                )
            )
            own_copies[-1].start()

    barrier = pltpu.get_barrier_semaphore()
    for n in range(1, n_ga):
        pl.semaphore_signal(barrier, inc=1, device_id={"ga": ahead(n)}, device_id_type=MESH)
    for n in range(1, n_band):
        target = {"band": lax.rem(band + n, n_band)}
        pl.semaphore_signal(barrier, inc=1, device_id=target, device_id_type=MESH)
    pl.semaphore_wait(barrier, n_ga + n_band - 2)

    in_copies = [[], []]
    for h in range(2):
        for n in range(1, n_ga):
            peer = ahead(n)
            for c in range(2):
                copy = send(
                    coeffs_ref.at[bands(h, c), columns(peer)],
                    moved.at[h, n, part_rows(c)],
                    in_sems,
                    (h, n, c),
                    {"ga": peer},
                )
                copy.start()
                in_copies[h].append(copy)

    slot_ids = lax.broadcasted_iota(jnp.int32, mask.shape, 1)
    mask[...] = jnp.where(slot_ids < waves_ref[0], 1.0, 0.0)
    atoms = counts_ref.shape[1]
    counts = jnp.broadcast_to(counts_ref[...].astype(jnp.float32), (atoms, atoms))
    lane_ids = lax.broadcasted_iota(jnp.int32, (atoms, atoms), 1)
    row_ids = lax.broadcasted_iota(jnp.int32, (atoms, atoms), 0)
    starts = jnp.sum(jnp.where(lane_ids < row_ids, counts, 0.0), axis=1, keepdims=True)
    lengths = jnp.sum(jnp.where(lane_ids == row_ids, counts, 0.0), axis=1, keepdims=True)
    most = coupling_ref.shape[0]
    narrow = tile // 2
    spread = jnp.where(
        lax.broadcasted_iota(jnp.int32, (narrow, tile), 1) // 2
        == lax.broadcasted_iota(jnp.int32, (narrow, tile), 0),
        1.0,
        0.0,
    )

    def weights_of(t, carry):
        at = pl.ds(pl.multiple_of(t * tile, tile), tile)
        halved = coupling_ref[:, pl.ds(pl.multiple_of(t * narrow, narrow), narrow)]
        pairs = jnp.dot(
            halved, spread, precision=lax.Precision.HIGHEST, preferred_element_type=jnp.float32
        )
        ids = t * narrow + lax.broadcasted_iota(jnp.int32, (atoms, tile), 1) // 2
        ids = ids.astype(jnp.float32)
        inside = (starts <= ids) & (ids < starts + lengths)
        first = jnp.sum(jnp.where(inside, starts, 0.0), axis=0, keepdims=True)
        length = jnp.sum(jnp.where(inside, lengths, 0.0), axis=0, keepdims=True)
        shape = (weights.shape[0], tile)
        shift = lax.broadcasted_iota(jnp.int32, shape, 0).astype(jnp.float32) - REACH
        place = shift + (ids[0:1] - first)
        sums = jnp.zeros(shape, jnp.float32)
        for k in range(most):
            row = jnp.where(k < length, pairs[k : k + 1], 0.0)
            sums = sums + jnp.where(place == k, row, 0.0)
        weights[:, at] = sums
        return carry

    lax.fori_loop(0, rows // tile, weights_of, 0)

    def even_lanes(shape):
        return lax.broadcasted_iota(jnp.int32, shape, len(shape) - 1) % 2 == 0

    def swapped(values, even):
        last = values.shape[-1]
        dim = len(values.shape) - 1
        return jnp.where(even, pltpu.roll(values, last - 1, dim), pltpu.roll(values, 1, dim))

    def project_half(h):
        for copy in own_copies[2 * h : 2 * h + 2]:
            copy.wait()
        for copy in in_copies[h]:
            copy.wait_recv()
        seen = mask[0:1, :].astype(jnp.bfloat16)
        lhs[...] = moved[h].reshape(lhs.shape) * seen

        def project(t, carry):
            at = pl.ds(pl.multiple_of(t * tile, tile), tile)
            sums = lax.dot_general(
                lhs[...],
                beta[at, :],
                (((1,), (1,)), ((), ())),
                preferred_element_type=jnp.float32,
            ).reshape(n_ga, 2, half, tile)
            even = even_lanes((n_ga, half, tile))
            real, imag = sums[:, 0], sums[:, 1]
            pairs = jnp.where(even, real, -real) + swapped(imag, even)
            part[h, :, :, at] = pairs.astype(jnp.bfloat16)
            return carry

        lax.fori_loop(0, rows // tile, project, 0)
        copies = [None]
        for n in range(1, n_ga):
            copies.append(
                send(part.at[h, n], parts_in.at[h, n], part_sems, (h, n), {"ga": behind(n)})
            )
            copies[n].start()
        return copies

    def couple_half(h, part_copies):
        summed = part[h, 0].astype(jnp.float32)
        for n in range(1, n_ga):
            part_copies[n].wait_recv()
            summed = summed + parts_in[h, n].astype(jnp.float32)
        coupled = jnp.zeros_like(summed)
        for d in range(-REACH, REACH + 1):
            moved_by = pltpu.roll(summed, (-2 * d) % rows, 1) if d else summed
            coupled = coupled + weights[d + REACH : d + REACH + 1, :] * moved_by
        mixed[h] = coupled.astype(jnp.bfloat16)
        mixed_in[h, 0] = mixed[h]
        copies = [None]
        for n in range(1, n_ga):
            copies.append(
                send(mixed.at[h], mixed_in.at[h, n], mixed_sems, (h, n), {"ga": ahead(n)})
            )
            copies[n].start()
        terms = jnp.sum(summed * coupled, axis=1, keepdims=True) / (rows // 2)
        diagonal = lax.broadcasted_iota(
            jnp.int32, (half, 128), 0
        ) + h * half == lax.broadcasted_iota(jnp.int32, (half, 128), 1)
        return copies, jnp.sum(jnp.where(diagonal, terms, 0.0), axis=0, keepdims=True)

    def apply_half(h, mixed_copies):
        for n in range(1, n_ga):
            mixed_copies[n].wait_recv()

        def operand(n, carry):
            values = mixed_in[h, n].astype(jnp.float32)
            even = even_lanes(values.shape)
            both = jnp.concatenate(
                [jnp.where(even, values, -values), swapped(values, even)], axis=0
            )
            lhs[pl.ds(pl.multiple_of(n * own, own), own), :] = both.astype(jnp.bfloat16)
            return carry

        lax.fori_loop(0, n_ga, operand, 0)

        def apply(t, carry):
            at = pl.ds(pl.multiple_of(t * tile, tile), tile)
            sums = jnp.dot(lhs[...], beta[:, at], preferred_element_type=jnp.float32)
            sums = sums * mask[0:1, at]
            prod[h, :, :, at] = sums.astype(jnp.bfloat16).reshape(n_ga, own, tile)
            return carry

        lax.fori_loop(0, slots // tile, apply, 0)
        copies = []
        for n in range(1, n_ga):
            for c in range(2):
                copies.append(
                    send(
                        prod.at[h, n, part_rows(c)],
                        out_ref.at[bands(h, c), columns(ga)],
                        out_sems,
                        (h, n, c),
                        {"ga": behind(n)},
                    )
                )
                copies[-1].start()
        kept = []
        for c in range(2):
            kept.append(
                pltpu.make_async_copy(
                    prod.at[h, 0, part_rows(c)],
                    out_ref.at[bands(h, c), columns(ga)],
                    own_sem.at[2 + h, c],
                )
            )
            kept[-1].start()
        return copies, kept

    beta_copy.wait()
    first_parts = project_half(0)
    second_parts = project_half(1)
    first_mixed, first_terms = couple_half(0, first_parts)
    second_mixed, second_terms = couple_half(1, second_parts)
    terms = first_terms + second_terms
    energy_ref[...] = terms[0, :own]
    own_energy[...] = jnp.broadcast_to(jnp.sum(terms, axis=1, keepdims=True), own_energy.shape)
    energy_copies = []
    for n in range(1, n_ga):
        energy_copies.append(
            send(own_energy, energy_in.at[ga], energy_sems, (n,), {"ga": ahead(n)})
        )
        energy_copies[-1].start()
    first_out, first_kept = apply_half(0, first_mixed)
    second_out, second_kept = apply_half(1, second_mixed)

    for copy in energy_copies:
        copy.wait_recv()
    energy_in[pl.ds(ga, 1)] = own_energy[...][None]
    sums = energy_in[0]
    for n in range(1, n_ga):
        sums = sums + energy_in[n]
    group_energy[...] = sums
    band_copies = []
    for n in range(1, n_band):
        target = {"band": lax.rem(band + n, n_band)}
        band_copies.append(send(group_energy, band_in.at[band], band_sems, (n,), target))
        band_copies[-1].start()
    for copy in band_copies:
        copy.wait_recv()
    band_in[pl.ds(band, 1)] = sums[None]
    sums = band_in[0]
    for n in range(1, n_band):
        sums = sums + band_in[n]
    total_ref[...] = sums[0:1, 0:1] / math.sqrt(own * n_ga * n_band)

    for copy in first_kept + second_kept:
        copy.wait()
    for copy in first_out + second_out:
        copy.wait_recv()
    sent = first_parts[1:] + second_parts[1:] + first_mixed[1:] + second_mixed[1:]
    for copy in in_copies[0] + in_copies[1] + sent + first_out + second_out:
        copy.wait_send()
    for copy in energy_copies + band_copies:
        copy.wait_send()


def shards(coeffs, projectors, block_coupling, atom_counts, wave_counts):
    parts, own, slots_all = coeffs.shape
    rows = projectors.shape[0] * parts
    slots = projectors.shape[2]
    n_ga = lax.axis_size("ga")
    n_band = lax.axis_size("band")
    low, full = jnp.bfloat16, jnp.float32
    vmem = pl.BlockSpec(memory_space=pltpu.VMEM)
    anywhere = pl.BlockSpec(memory_space=pl.ANY)
    applied, energy, total = pl.pallas_call(
        kernel,
        out_shape=[
            jax.ShapeDtypeStruct((parts * own, slots_all), low),
            jax.ShapeDtypeStruct((own,), full),
            jax.ShapeDtypeStruct((1, 1), full),
        ],
        in_specs=[vmem, pl.BlockSpec(memory_space=pltpu.SMEM), vmem, anywhere, anywhere],
        out_specs=[anywhere, vmem, vmem],
        scratch_shapes=[
            pltpu.VMEM((rows, slots), low),
            pltpu.VMEM((2, n_ga, own, slots), low),
            pltpu.VMEM((n_ga * own, slots), low),
            pltpu.VMEM((2, n_ga, own // 2, rows), low),
            pltpu.VMEM((2, n_ga, own // 2, rows), low),
            pltpu.VMEM((2, own // 2, rows), low),
            pltpu.VMEM((2, n_ga, own // 2, rows), low),
            pltpu.VMEM((2, n_ga, own, slots), low),
            pltpu.VMEM((40, rows), full),
            pltpu.VMEM((8, slots), full),
            pltpu.VMEM((8, 128), full),
            pltpu.VMEM((n_ga, 8, 128), full),
            pltpu.VMEM((8, 128), full),
            pltpu.VMEM((n_band, 8, 128), full),
            pltpu.SemaphoreType.DMA,
            pltpu.SemaphoreType.DMA((4, 2)),
            pltpu.SemaphoreType.DMA((2, 2, n_ga, 2)),
            pltpu.SemaphoreType.DMA((2, 2, n_ga)),
            pltpu.SemaphoreType.DMA((2, 2, n_ga)),
            pltpu.SemaphoreType.DMA((2, 2, n_ga, 2)),
            pltpu.SemaphoreType.DMA((2, n_ga)),
            pltpu.SemaphoreType.DMA((2, n_band)),
        ],
        compiler_params=pltpu.CompilerParams(
            collective_id=0, has_side_effects=True, vmem_limit_bytes=56 << 20
        ),
    )(
        atom_counts.reshape(1, -1),
        wave_counts,
        block_coupling.T,
        coeffs.reshape(parts * own, slots_all),
        projectors,
    )
    return applied.reshape(coeffs.shape), energy, total[0, 0]


def solution(mesh):
    return jax.shard_map(
        shards,
        mesh=mesh,
        in_specs=(P(None, ("ga", "band"), None), P(None, None, "ga"), P(), P(), P("ga")),
        out_specs=(P(None, ("ga", "band"), None), P(("ga", "band")), P()),
        check_vma=False,
    )
```

time: 131 us -> 115 us (0.88)
  the two profiles are of different devices: /device:TPU:14 before, /device:TPU:0 now
where the time goes in v2:
time: 115 us
  Pallas kernels  108 us (94%)
  local copies, waits for them, and re-layouts  3.92 us (3%)
  between operations  3.09 us (3%)
    pallas_call x1, Pallas kernels, shards(): pl.pallas_call(kernel, out_shape=[jax.ShapeDtypeStruct((parts * own, slot...  108 us
    unnamed x4, local copies, waits for them, and re-layouts  3.92 us

profile of v2, /device:TPU:0, one launch (start us, length us, event | category | flops | bytes accessed | tf_op | source)
XLA Modules:
  0.0 114.6 jit_solution(11417307430743558063)
XLA Ops:
  1.3 107.6 %shard_map.76 = (bf16[32,40960]{1,0:T(8,128)(2,1)}, f32[16]{0:T(128)}, f32[1,1]{1,0:T(1,128)}) custom-call(s32[1,160]{1,0:T(1,128)} %bitcast.8, s32[1]{0:T(128)S(6)} %copy.11.waves_ref, f32[18,1280]{1,0:T(8,128)} %bitcast.7, bf16[32,40960]{1,0:T(8,128)(2,1)} %bitcast.6, bf16[1280,2,2560]{2,1,0:T(2,128)(2,1)} %proj_ref.1), custom_call_target="tpu_custom_call" | custom-call | tf_op jit(solution)/shard_map/pallas_call | solution.py:342
  108.9 0.0 copy-start
  108.9 3.4 %copy.12 = bf16[2,16,40960]{2,1,0:T(8,128)(2,1)} copy(bf16[2,16,40960]{2,1,0:T(8,128)(2,1)} %bitcast.5) | data formatting | bytes 5242880
  112.3 0.0 copy-done
  112.3 0.5 copy.13
Async XLA Ops:
  108.9 3.4 %copy-start = (f32[16]{0:T(128)S(1)}, f32[16]{0:T(128)}, u32[]{:S(2)}) copy-start(f32[16]{0:T(128)} %get-tuple-element.13) | copy-start | bytes 196

commit v3 on v2

--- a/solution.py
+++ b/solution.py
@@ -11,27 +11,27 @@
 SIDE = 4
 REACH = 17
 
-PLACES = [(0, 0)] + sorted(
-    [(dx, dz) for dx in range(SIDE) for dz in range(SIDE) if (dx, dz) != (0, 0)],
-    key=lambda o: min(o[0], SIDE - o[0]) + min(o[1], SIDE - o[1]),
-)
+PLACES = [(dx, dz) for dx in range(SIDE) for dz in range(SIDE)]
+NEAR = sorted(PLACES[1:], key=lambda o: min(o[0], SIDE - o[0]) + min(o[1], SIDE - o[1]))
 
 
 def kernel(
-    counts_ref,
-    waves_ref,
-    coupling_ref,
+    counts_hbm,
+    waves_hbm,
+    coupling_hbm,
     coeffs_ref,
     proj_ref,
     out_ref,
     energy_ref,
     total_ref,
     beta,
+    turned,
     moved,
     lhs,
     part,
     parts_in,
-    mixed,
+    line,
+    line_in,
     mixed_in,
     prod,
     weights,
@@ -40,18 +40,25 @@
     energy_in,
     group_energy,
     band_in,
+    counts_ref,
+    waves_ref,
+    coupling_ref,
+    small_sems,
     beta_sem,
     own_sem,
     in_sems,
     part_sems,
+    line_sems,
     mixed_sems,
+    row_sems,
     out_sems,
     energy_sems,
     band_sems,
 ):
     n_ga = len(PLACES)
     n_band = lax.axis_size("band")
-    half = mixed.shape[1]
+    half = part.shape[4]
+    lanes = part.shape[5]
     own = 2 * half
     slots = moved.shape[3]
     rows = beta.shape[0]
@@ -60,12 +67,10 @@
     band = lax.axis_index("band")
     gx, gz = ga // SIDE, ga % SIDE
 
-    def ahead(n):
-        dx, dz = PLACES[n]
+    def ahead(dx, dz):
         return lax.rem(gx + dx, SIDE) * SIDE + lax.rem(gz + dz, SIDE)
 
-    def behind(n):
-        dx, dz = PLACES[n]
+    def behind(dx, dz):
         return lax.rem(gx + SIDE - dx, SIDE) * SIDE + lax.rem(gz + SIDE - dz, SIDE)
 
     def columns(index):
@@ -109,9 +114,17 @@
             )
             own_copies[-1].start()
 
+    small_copies = [
+        pltpu.make_async_copy(counts_hbm, counts_ref, small_sems.at[0]),
+        pltpu.make_async_copy(waves_hbm, waves_ref, small_sems.at[1]),
+        pltpu.make_async_copy(coupling_hbm, coupling_ref, small_sems.at[2]),
+    ]
+    for copy in small_copies:
+        copy.start()
+
     barrier = pltpu.get_barrier_semaphore()
     for n in range(1, n_ga):
-        pl.semaphore_signal(barrier, inc=1, device_id={"ga": ahead(n)}, device_id_type=MESH)
+        pl.semaphore_signal(barrier, inc=1, device_id={"ga": ahead(*PLACES[n])}, device_id_type=MESH)
     for n in range(1, n_band):
         target = {"band": lax.rem(band + n, n_band)}
         pl.semaphore_signal(barrier, inc=1, device_id=target, device_id_type=MESH)
@@ -119,8 +132,8 @@
 
     in_copies = [[], []]
     for h in range(2):
-        for n in range(1, n_ga):
-            peer = ahead(n)
+        for dx, dz in NEAR:
+            peer, n = ahead(dx, dz), dx * SIDE + dz
             for c in range(2):
                 copy = send(
                     coeffs_ref.at[bands(h, c), columns(peer)],
@@ -132,6 +145,8 @@
                 copy.start()
                 in_copies[h].append(copy)
 
+    for copy in small_copies:
+        copy.wait()
     slot_ids = lax.broadcasted_iota(jnp.int32, mask.shape, 1)
     mask[...] = jnp.where(slot_ids < waves_ref[0], 1.0, 0.0)
     atoms = counts_ref.shape[1]
@@ -180,7 +195,10 @@
         dim = len(values.shape) - 1
         return jnp.where(even, pltpu.roll(values, last - 1, dim), pltpu.roll(values, 1, dim))
 
-    def project_half(h):
+    def place(side, first, second):
+        return (first, second) if side == 0 else (second, first)
+
+    def take_half(h):
         for copy in own_copies[2 * h : 2 * h + 2]:
             copy.wait()
         for copy in in_copies[h]:
@@ -188,58 +206,115 @@
         seen = mask[0:1, :].astype(jnp.bfloat16)
         lhs[...] = moved[h].reshape(lhs.shape) * seen
 
-        def project(t, carry):
-            at = pl.ds(pl.multiple_of(t * tile, tile), tile)
-            sums = lax.dot_general(
-                lhs[...],
-                beta[at, :],
-                (((1,), (1,)), ((), ())),
-                preferred_element_type=jnp.float32,
-            ).reshape(n_ga, 2, half, tile)
-            even = even_lanes((n_ga, half, tile))
-            real, imag = sums[:, 0], sums[:, 1]
-            pairs = jnp.where(even, real, -real) + swapped(imag, even)
-            part[h, :, :, at] = pairs.astype(jnp.bfloat16)
-            return carry
-
-        lax.fori_loop(0, rows // tile, project, 0)
+    def project_side(h, side):
+        sums = jnp.dot(
+            lhs[...],
+            turned[:, side * lanes : (side + 1) * lanes],
+            preferred_element_type=jnp.float32,
+        ).reshape(n_ga, 2, half, lanes)
+        even = even_lanes((half, lanes))
+        for first in range(SIDE):
+            for second in range(SIDE):
+                dx, dz = place(side, first, second)
+                real, imag = sums[dx * SIDE + dz, 0], sums[dx * SIDE + dz, 1]
+                pairs = jnp.where(even, real, -real) + swapped(imag, even)
+                part[h, side, first, second] = pairs.astype(jnp.bfloat16)
         copies = [None]
-        for n in range(1, n_ga):
+        for k in range(1, SIDE):
             copies.append(
-                send(part.at[h, n], parts_in.at[h, n], part_sems, (h, n), {"ga": behind(n)})
+                send(
+                    part.at[h, side, k],
+                    parts_in.at[h, side, k],
+                    part_sems,
+                    (h, side, k),
+                    {"ga": behind(*place(side, k, 0))},
+                )
             )
-            copies[n].start()
+            copies[k].start()
         return copies
 
-    def couple_half(h, part_copies):
-        summed = part[h, 0].astype(jnp.float32)
-        for n in range(1, n_ga):
-            part_copies[n].wait_recv()
-            summed = summed + parts_in[h, n].astype(jnp.float32)
+    def sum_line(h, side, part_copies):
+        summed = part[h, side, 0].astype(jnp.float32)
+        for k in range(1, SIDE):
+            part_copies[k].wait_recv()
+            summed = summed + parts_in[h, side, k].astype(jnp.float32)
+        line[h, side] = summed.astype(jnp.bfloat16)
+        copies = [None]
+        for k in range(1, SIDE):
+            copies.append(
+                send(
+                    line.at[h, side, k],
+                    line_in.at[h, side, k],
+                    line_sems,
+                    (h, side, k),
+                    {"ga": behind(*place(side, 0, k))},
+                )
+            )
+            copies[k].start()
+        return copies
+
+    def couple_half(h, line_copies):
+        sides = []
+        for side in range(2):
+            summed = line[h, side, 0].astype(jnp.float32)
+            for k in range(1, SIDE):
+                line_copies[side][k].wait_recv()
+                summed = summed + line_in[h, side, k].astype(jnp.float32)
+            sides.append(summed)
+        summed = jnp.concatenate(sides, axis=1)
         coupled = jnp.zeros_like(summed)
         for d in range(-REACH, REACH + 1):
             moved_by = pltpu.roll(summed, (-2 * d) % rows, 1) if d else summed
             coupled = coupled + weights[d + REACH : d + REACH + 1, :] * moved_by
-        mixed[h] = coupled.astype(jnp.bfloat16)
-        mixed_in[h, 0] = mixed[h]
-        copies = [None]
-        for n in range(1, n_ga):
-            copies.append(
-                send(mixed.at[h], mixed_in.at[h, n], mixed_sems, (h, n), {"ga": ahead(n)})
-            )
-            copies[n].start()
+        low = coupled.astype(jnp.bfloat16)
+        copies = []
+        for side in range(2):
+            mixed_in[h, side, 0, 0] = low[:, side * lanes : (side + 1) * lanes]
+            copies.append([None])
+            for k in range(1, SIDE):
+                copies[side].append(
+                    send(
+                        mixed_in.at[h, side, 0, 0],
+                        mixed_in.at[h, side, 0, k],
+                        mixed_sems,
+                        (h, side, k),
+                        {"ga": ahead(*place(side, k, 0))},
+                    )
+                )
+                copies[side][k].start()
         terms = jnp.sum(summed * coupled, axis=1, keepdims=True) / (rows // 2)
         diagonal = lax.broadcasted_iota(
             jnp.int32, (half, 128), 0
         ) + h * half == lax.broadcasted_iota(jnp.int32, (half, 128), 1)
         return copies, jnp.sum(jnp.where(diagonal, terms, 0.0), axis=0, keepdims=True)
 
-    def apply_half(h, mixed_copies):
-        for n in range(1, n_ga):
-            mixed_copies[n].wait_recv()
+    def pass_on(h, mixed_copies):
+        copies = []
+        for side in range(2):
+            for k in range(1, SIDE):
+                mixed_copies[side][k].wait_recv()
+            for k in range(1, SIDE):
+                copies.append(
+                    send(
+                        mixed_in.at[h, side, 0],
+                        mixed_in.at[h, side, k],
+                        row_sems,
+                        (h, side, k),
+                        {"ga": ahead(*place(side, 0, k))},
+                    )
+                )
+                copies[-1].start()
+        return copies
+
+    def operand_half(h, row_copies):
+        for copy in row_copies:
+            copy.wait_recv()
 
         def operand(n, carry):
-            values = mixed_in[h, n].astype(jnp.float32)
+            dx, dz = n // SIDE, lax.rem(n, SIDE)
+            values = jnp.concatenate(
+                [mixed_in[h, 0, dz, dx], mixed_in[h, 1, dx, dz]], axis=1
+            ).astype(jnp.float32)
             even = even_lanes(values.shape)
             both = jnp.concatenate(
                 [jnp.where(even, values, -values), swapped(values, even)], axis=0
@@ -249,55 +324,99 @@
 
         lax.fori_loop(0, n_ga, operand, 0)
 
-        def apply(t, carry):
-            at = pl.ds(pl.multiple_of(t * tile, tile), tile)
-            sums = jnp.dot(lhs[...], beta[:, at], preferred_element_type=jnp.float32)
-            sums = sums * mask[0:1, at]
-            prod[h, :, :, at] = sums.astype(jnp.bfloat16).reshape(n_ga, own, tile)
-            return carry
-
-        lax.fori_loop(0, slots // tile, apply, 0)
-        copies = []
-        for n in range(1, n_ga):
+    def apply_part(h, q):
+        cut = slots // 2
+        at = pl.ds(q * cut, cut)
+        sums = jnp.dot(lhs[...], beta[:, at], preferred_element_type=jnp.float32)
+        sums = sums * mask[0:1, at]
+        prod[h, :, :, at] = sums.astype(jnp.bfloat16).reshape(n_ga, own, cut)
+
+    def to_owner(src, dst, target):
+        return pltpu.make_async_remote_copy(
+            src,
+            dst,
+            out_sems.at[0],
+            out_sems.at[1],
+            device_id={"ga": target},
+            device_id_type=MESH,
+        )
+
+    def return_part(h, q):
+        cut = slots // 2
+        here = pl.ds(q * cut, cut)
+        there = pl.ds(pl.multiple_of(ga * slots + q * cut, 128), cut)
+        kept = []
+        for dx, dz in NEAR:
+            n = dx * SIDE + dz
             for c in range(2):
-                copies.append(
-                    send(
-                        prod.at[h, n, part_rows(c)],
-                        out_ref.at[bands(h, c), columns(ga)],
-                        out_sems,
-                        (h, n, c),
-                        {"ga": behind(n)},
-                    )
-                )
-                copies[-1].start()
-        kept = []
+                to_owner(
+                    prod.at[h, n, part_rows(c), here],
+                    out_ref.at[bands(h, c), there],
+                    behind(dx, dz),
+                ).start()
         for c in range(2):
             kept.append(
                 pltpu.make_async_copy(
-                    prod.at[h, 0, part_rows(c)],
-                    out_ref.at[bands(h, c), columns(ga)],
-                    own_sem.at[2 + h, c],
+                    prod.at[h, 0, part_rows(c), here],
+                    out_ref.at[bands(h, c), there],
+                    own_sem.at[2 + 2 * h + q, c],
                 )
             )
             kept[-1].start()
-        return copies, kept
+        return kept
 
     beta_copy.wait()
-    first_parts = project_half(0)
-    second_parts = project_half(1)
-    first_mixed, first_terms = couple_half(0, first_parts)
-    second_mixed, second_terms = couple_half(1, second_parts)
+    unit = jnp.where(
+        lax.broadcasted_iota(jnp.int32, (tile, tile), 0)
+        == lax.broadcasted_iota(jnp.int32, (tile, tile), 1),
+        1.0,
+        0.0,
+    ).astype(jnp.bfloat16)
+    tiles = slots // tile
+
+    def turn(t, carry):
+        here = pl.ds(pl.multiple_of(t * tile, tile), tile)
+        for u in range(tiles):
+            there = pl.ds(u * tile, tile)
+            turned[there, here] = lax.dot_general(
+                unit,
+                beta[here, there],
+                (((1,), (1,)), ((), ())),
+                preferred_element_type=jnp.float32,
+            ).astype(jnp.bfloat16)
+        return carry
+
+    lax.fori_loop(0, rows // tile, turn, 0)
+    take_half(0)
+    parts0 = [project_side(0, 0), project_side(0, 1)]
+    take_half(1)
+    parts1 = [project_side(1, 0)]
+    lines0 = [sum_line(0, 0, parts0[0]), sum_line(0, 1, parts0[1])]
+    parts1.append(project_side(1, 1))
+    mixed0, first_terms = couple_half(0, lines0)
+    lines1 = [sum_line(1, 0, parts1[0]), sum_line(1, 1, parts1[1])]
+    rows0 = pass_on(0, mixed0)
+    mixed1, second_terms = couple_half(1, lines1)
     terms = first_terms + second_terms
     energy_ref[...] = terms[0, :own]
     own_energy[...] = jnp.broadcast_to(jnp.sum(terms, axis=1, keepdims=True), own_energy.shape)
     energy_copies = []
     for n in range(1, n_ga):
         energy_copies.append(
-            send(own_energy, energy_in.at[ga], energy_sems, (n,), {"ga": ahead(n)})
+            send(own_energy, energy_in.at[ga], energy_sems, (n,), {"ga": ahead(*PLACES[n])})
         )
         energy_copies[-1].start()
-    first_out, first_kept = apply_half(0, first_mixed)
-    second_out, second_kept = apply_half(1, second_mixed)
+    operand_half(0, rows0)
+    apply_part(0, 0)
+    rows1 = pass_on(1, mixed1)
+    returned = [return_part(0, 0)]
+    apply_part(0, 1)
+    returned.append(return_part(0, 1))
+    operand_half(1, rows1)
+    apply_part(1, 0)
+    returned.append(return_part(1, 0))
+    apply_part(1, 1)
+    returned.append(return_part(1, 1))
 
     for copy in energy_copies:
         copy.wait_recv()
@@ -319,15 +438,18 @@
         sums = sums + band_in[n]
     total_ref[...] = sums[0:1, 0:1] / math.sqrt(own * n_ga * n_band)
 
-    for copy in first_kept + second_kept:
-        copy.wait()
-    for copy in first_out + second_out:
-        copy.wait_recv()
-    sent = first_parts[1:] + second_parts[1:] + first_mixed[1:] + second_mixed[1:]
-    for copy in in_copies[0] + in_copies[1] + sent + first_out + second_out:
+    sent = rows0 + rows1
+    for copies in parts0 + parts1 + lines0 + lines1 + mixed0 + mixed1:
+        sent = sent + copies[1:]
+    for copy in in_copies[0] + in_copies[1] + sent + energy_copies + band_copies:
         copy.wait_send()
-    for copy in energy_copies + band_copies:
-        copy.wait_send()
+    for kept in returned:
+        for copy in kept:
+            copy.wait()
+    everything = prod.at[:, pl.ds(1, n_ga - 1)]
+    whole = to_owner(everything, everything, behind(0, 1))
+    whole.wait_recv()
+    whole.wait_send()
 
 
 def shards(coeffs, projectors, block_coupling, atom_counts, wave_counts):
@@ -346,16 +468,18 @@
             jax.ShapeDtypeStruct((own,), full),
             jax.ShapeDtypeStruct((1, 1), full),
         ],
-        in_specs=[vmem, pl.BlockSpec(memory_space=pltpu.SMEM), vmem, anywhere, anywhere],
+        in_specs=[anywhere] * 5,
         out_specs=[anywhere, vmem, vmem],
         scratch_shapes=[
             pltpu.VMEM((rows, slots), low),
+            pltpu.VMEM((slots, rows), low),
             pltpu.VMEM((2, n_ga, own, slots), low),
             pltpu.VMEM((n_ga * own, slots), low),
-            pltpu.VMEM((2, n_ga, own // 2, rows), low),
-            pltpu.VMEM((2, n_ga, own // 2, rows), low),
-            pltpu.VMEM((2, own // 2, rows), low),
-            pltpu.VMEM((2, n_ga, own // 2, rows), low),
+            pltpu.VMEM((2, 2, SIDE, SIDE, own // 2, rows // 2), low),
+            pltpu.VMEM((2, 2, SIDE, SIDE, own // 2, rows // 2), low),
+            pltpu.VMEM((2, 2, SIDE, own // 2, rows // 2), low),
+            pltpu.VMEM((2, 2, SIDE, own // 2, rows // 2), low),
+            pltpu.VMEM((2, 2, SIDE, SIDE, own // 2, rows // 2), low),
             pltpu.VMEM((2, n_ga, own, slots), low),
             pltpu.VMEM((40, rows), full),
             pltpu.VMEM((8, slots), full),
@@ -363,12 +487,18 @@
             pltpu.VMEM((n_ga, 8, 128), full),
             pltpu.VMEM((8, 128), full),
             pltpu.VMEM((n_band, 8, 128), full),
+            pltpu.VMEM((1, atom_counts.shape[0]), jnp.int32),
+            pltpu.SMEM((1,), jnp.int32),
+            pltpu.VMEM(block_coupling.shape[::-1], full),
+            pltpu.SemaphoreType.DMA((3,)),
             pltpu.SemaphoreType.DMA,
-            pltpu.SemaphoreType.DMA((4, 2)),
+            pltpu.SemaphoreType.DMA((6, 2)),
             pltpu.SemaphoreType.DMA((2, 2, n_ga, 2)),
-            pltpu.SemaphoreType.DMA((2, 2, n_ga)),
-            pltpu.SemaphoreType.DMA((2, 2, n_ga)),
-            pltpu.SemaphoreType.DMA((2, 2, n_ga, 2)),
+            pltpu.SemaphoreType.DMA((2, 2, 2, SIDE)),
+            pltpu.SemaphoreType.DMA((2, 2, 2, SIDE)),
+            pltpu.SemaphoreType.DMA((2, 2, 2, SIDE)),
+            pltpu.SemaphoreType.DMA((2, 2, 2, SIDE)),
+            pltpu.SemaphoreType.DMA((2,)),
             pltpu.SemaphoreType.DMA((2, n_ga)),
             pltpu.SemaphoreType.DMA((2, n_band)),
         ],

time: 115 us -> 106 us (0.922)
  Pallas kernels: 108 us -> 98.7 us
    pallas_call x1, Pallas kernels: 108 us -> 98.7 us  [shards(): pl.pallas_call(kernel, out_shape=[jax.ShapeDtypeStruct((parts * own, slot...]
where the time goes in v3:
time: 106 us
  Pallas kernels  98.7 us (93%)
  local copies, waits for them, and re-layouts  3.92 us (4%)
  between operations  3.09 us (3%)
    pallas_call x1, Pallas kernels, shards(): pl.pallas_call(kernel, out_shape=[jax.ShapeDtypeStruct((parts * own, slot...  98.7 us
    unnamed x4, local copies, waits for them, and re-layouts  3.92 us

profile of v3, /device:TPU:0, one launch (start us, length us, event | category | flops | bytes accessed | tf_op | source)
XLA Modules:
  0.0 105.7 jit_solution(8174038596236520499)
XLA Ops:
  1.3 98.7 %shard_map.76 = (bf16[32,40960]{1,0:T(8,128)(2,1)}, f32[16]{0:T(128)}, f32[1,1]{1,0:T(1,128)}) custom-call(s32[1,160]{1,0:T(1,128)} %bitcast.8, s32[1]{0:T(128)S(6)} %copy.11.waves_hbm, f32[18,1280]{1,0:T(8,128)} %bitcast.7, bf16[32,40960]{1,0:T(8,128)(2,1)} %bitcast.6, bf16[1280,2,2560]{2,1,0:T(2,128)(2,1)} %proj_ref.1), custom_call_target="tpu_custom_call" | custom-call | tf_op jit(solution)/shard_map/pallas_call | solution.py:464
  99.9 0.0 copy-start
  99.9 3.4 %copy.12 = bf16[2,16,40960]{2,1,0:T(8,128)(2,1)} copy(bf16[2,16,40960]{2,1,0:T(8,128)(2,1)} %bitcast.5) | data formatting | bytes 5242880
  103.3 0.0 copy-done
  103.4 0.5 copy.13
Async XLA Ops:
  99.9 3.4 %copy-start = (f32[16]{0:T(128)S(1)}, f32[16]{0:T(128)}, u32[]{:S(2)}) copy-start(f32[16]{0:T(128)} %get-tuple-element.13) | copy-start | bytes 196

commit v4 on v3

--- a/solution.py
+++ b/solution.py
@@ -452,6 +452,26 @@
     whole.wait_send()
 
 
+def deliver(applied_ref, energy_ref, total_ref, applied_out, energy_out, total_out, row, one, sems):
+    pieces = sems.shape[0] - 4
+    cut = applied_ref.shape[1] // pieces
+    copies = []
+    for k in range(pieces):
+        at = pl.ds(k * cut, cut)
+        copies.append(pltpu.make_async_copy(applied_ref.at[:, at], applied_out.at[:, at], sems.at[k]))
+        copies[k].start()
+    small = ((energy_ref, row, energy_out, pieces), (total_ref, one, total_out, pieces + 2))
+    ins = [pltpu.make_async_copy(ref, kept, sems.at[k]) for ref, kept, _, k in small]
+    outs = [pltpu.make_async_copy(kept, out, sems.at[k + 1]) for _, kept, out, k in small]
+    for copy in ins:
+        copy.start()
+    for before, after in zip(ins, outs):
+        before.wait()
+        after.start()
+    for copy in copies + outs:
+        copy.wait()
+
+
 def shards(coeffs, projectors, block_coupling, atom_counts, wave_counts):
     parts, own, slots_all = coeffs.shape
     rows = projectors.shape[0] * parts
@@ -464,12 +484,12 @@
     applied, energy, total = pl.pallas_call(
         kernel,
         out_shape=[
-            jax.ShapeDtypeStruct((parts * own, slots_all), low),
+            pltpu.VMEM((parts * own, slots_all), low),
             jax.ShapeDtypeStruct((own,), full),
             jax.ShapeDtypeStruct((1, 1), full),
         ],
         in_specs=[anywhere] * 5,
-        out_specs=[anywhere, vmem, vmem],
+        out_specs=[vmem, vmem, vmem],
         scratch_shapes=[
             pltpu.VMEM((rows, slots), low),
             pltpu.VMEM((slots, rows), low),
@@ -512,6 +532,20 @@
         coeffs.reshape(parts * own, slots_all),
         projectors,
     )
+    shapes = [jax.ShapeDtypeStruct(x.shape, x.dtype) for x in (applied, energy, total)]
+    pieces = 8
+    applied, energy, total = pl.pallas_call(
+        deliver,
+        out_shape=shapes,
+        in_specs=[vmem, anywhere, anywhere],
+        out_specs=[anywhere] * 3,
+        scratch_shapes=[
+            pltpu.VMEM(energy.shape, full),
+            pltpu.VMEM(total.shape, full),
+            pltpu.SemaphoreType.DMA((pieces + 4,)),
+        ],
+        compiler_params=pltpu.CompilerParams(vmem_limit_bytes=56 << 20),
+    )(applied, energy, total)
     return applied.reshape(coeffs.shape), energy, total[0, 0]
 
 

time: 106 us -> 106 us (level)
  Pallas kernels: 98.7 us -> 102 us
  local copies, waits for them, and re-layouts: 3.92 us -> 1.5 us
  between operations: 3.09 us -> 1.46 us
    pallas_call x1 -> x2, Pallas kernels: 98.7 us -> 102 us  [the longest x1 98.4 us: shards(): pl.pallas_call(kernel, out_shape=[pltpu.VMEM((parts * own, slots_all), lo...]
    unnamed x4 -> x2, local copies, waits for them, and re-layouts: 3.92 us -> 1.5 us
where the time goes in v4:
time: 106 us; the launch traced here: 105 us
  Pallas kernels  102 us (96%)
  local copies, waits for them, and re-layouts  1.5 us (1%)
  between operations  1.46 us (1%)
    pallas_call x1, Pallas kernels, shards(): pl.pallas_call(kernel, out_shape=[pltpu.VMEM((parts * own, slots_all), lo...  98.4 us
    pallas_call x1, Pallas kernels, shards(): pl.pallas_call(deliver, out_shape=shapes, in_specs=[vmem, anywhere, anywh...  4.02 us

profile of v4, /device:TPU:0, one launch (start us, length us, event | category | flops | bytes accessed | tf_op | source)
XLA Modules:
  0.0 105.4 jit_solution(18087029288624783692)
XLA Ops:
  1.3 98.4 %shard_map.76 = (bf16[32,40960]{1,0:T(8,128)(2,1)S(1)}, f32[16]{0:T(128)}, f32[1,1]{1,0:T(1,128)}) custom-call(s32[1,160]{1,0:T(1,128)} %bitcast.7, s32[1]{0:T(128)S(6)} %copy.8.waves_hbm, f32[18,1280]{1,0:T(8,128)} %bitcast.6, bf16[32,40960]{1,0:T(8,128)(2,1)} %bitcast.5, bf16[1280,2,2560]{2,1,0:T(2,128)(2,1)} %proj_ref.1), custom_call_target="tpu_custom_call" | custom-call | tf_op jit(solution)/shard_map/pallas_call | solution.py:484
  99.7 0.0 copy-start
  99.7 1.5 %copy-done = bf16[32,40960]{1,0:T(8,128)(2,1)} copy-done((bf16[32,40960]{1,0:T(8,128)(2,1)}, bf16[32,40960]{1,0:T(8,128)(2,1)S(1)}, u32[]{:S(2)}) %copy-start) | copy-done | bytes 2621464
  101.2 4.0 %shard_map.77 = (bf16[32,40960]{1,0:T(8,128)(2,1)}, f32[16]{0:T(128)}, f32[1,1]{1,0:T(1,128)}) custom-call(bf16[32,40960]{1,0:T(8,128)(2,1)} %copy-done, f32[16]{0:T(128)} %get-tuple-element.10.energy_ref, f32[1,1]{1,0:T(1,128)} %get-tuple-element.11.total_ref), custom_call_target="tpu_custom_call" | custom-call | tf_op jit(solution)/shard_map/pallas_call | solution.py:537
Async XLA Ops:
  99.7 1.5 %copy-start = (bf16[32,40960]{1,0:T(8,128)(2,1)}, bf16[32,40960]{1,0:T(8,128)(2,1)S(1)}, u32[]{:S(2)}) copy-start(bf16[32,40960]{1,0:T(8,128)(2,1)S(1)} %get-tuple-element.9.applied_ref) | copy-start | bytes 7864324

commit v5 on v4

--- a/solution.py
+++ b/solution.py
@@ -545,7 +545,7 @@
             pltpu.SemaphoreType.DMA((pieces + 4,)),
         ],
         compiler_params=pltpu.CompilerParams(vmem_limit_bytes=56 << 20),
-    )(applied, energy, total)
+    )(pltpu.with_memory_space_constraint(applied, pltpu.VMEM), energy, total)
     return applied.reshape(coeffs.shape), energy, total[0, 0]
 
 

time: 106 us -> 102 us (0.962)
  local copies, waits for them, and re-layouts: 1.5 us -> 0 us
    pallas_call x1, Pallas kernels: 4.02 us -> 2.22 us  [shards(): pl.pallas_call(deliver, out_shape=shapes, in_specs=[vmem, anywhere, anywh...]
    unnamed x2 -> x0, local copies, waits for them, and re-layouts: 1.5 us -> none
where the time goes in v5:
time: 102 us
  Pallas kernels  101 us (99%)
  between operations  1.45 us (1%)
    pallas_call x1, Pallas kernels, shards(): pl.pallas_call(kernel, out_shape=[pltpu.VMEM((parts * own, slots_all), lo...  98.4 us
    pallas_call x1, Pallas kernels, shards(): pl.pallas_call(deliver, out_shape=shapes, in_specs=[vmem, anywhere, anywh...  2.22 us

profile of v5, /device:TPU:0, one launch (start us, length us, event | category | flops | bytes accessed | tf_op | source)
XLA Modules:
  0.0 102.0 jit_solution(2923958440907739585)
XLA Ops:
  1.3 98.4 %shard_map.76 = (bf16[32,40960]{1,0:T(8,128)(2,1)S(1)}, f32[16]{0:T(128)}, f32[1,1]{1,0:T(1,128)}) custom-call(s32[1,160]{1,0:T(1,128)} %bitcast.7, s32[1]{0:T(128)S(6)} %copy.8.waves_hbm, f32[18,1280]{1,0:T(8,128)} %bitcast.6, bf16[32,40960]{1,0:T(8,128)(2,1)} %bitcast.5, bf16[1280,2,2560]{2,1,0:T(2,128)(2,1)} %proj_ref.1), custom_call_target="tpu_custom_call" | custom-call | tf_op jit(solution)/shard_map/pallas_call | solution.py:484
  99.7 2.2 %shard_map.77 = (bf16[32,40960]{1,0:T(8,128)(2,1)}, f32[16]{0:T(128)}, f32[1,1]{1,0:T(1,128)}) custom-call(bf16[32,40960]{1,0:T(8,128)(2,1)S(1)} %get-tuple-element.9.applied_ref, f32[16]{0:T(128)} %get-tuple-element.10.energy_ref, f32[1,1]{1,0:T(1,128)} %get-tuple-element.11.total_ref), custom_call_target="tpu_custom_call" | custom-call | tf_op jit(solution)/shard_map/pallas_call | solution.py:537
